TPU v7x, 32 devices: a whole 2x2x4 slice. The times are simulated.
32 devices in a mesh: dp: 2 (over core), vocab: 16 (over z, y, x).
Axes of the slice: x: 2, y: 2, z: 4, core: 2. Of those that a mesh axis runs over, the one named last changes fastest.
Arguments:
- table: bfloat16 [16384, 4096], P('vocab'), may hold values from -0.75 to 0.75
- hidden: bfloat16 [512, 4096], P(('dp', 'vocab')), may hold values from -9 to 9
- cotangent: bfloat16 [512, 4096], P(('dp', 'vocab')), may hold values from -0.75 to 0.75
- input_ids: int32 [512], P('dp'), may hold values from 0 to 16383, as said below
- target_ids: int32 [512], P('dp'), may hold values from 0 to 16383
Outputs:
- table_grad: float32 [16384, 4096], P(('vocab', 'dp'))
- hidden_grad: bfloat16 [512, 4096], P(('dp', 'vocab'))
- token_loss: float32 [512], P('dp')
Inputs may be any that keep to these rules, and one draw needn't show every extreme that they name: `input_ids`: the ids of one replica group may all lie in the 1024 rows of one index of vocab; in every draw some group's ids do.
All inputs are finite; a program needn't handle non-finite values.
Results may differ from a plain program's by a relative error of at most 0.0034.
Values may be sent and summed in bfloat16 or wider, within the bound.
A program may use at most 128 MiB of HBM per device.

v0:
```python
import jax
import jax.numpy as jnp
from jax import lax
from jax.sharding import PartitionSpec as P


def shards(table, hidden, cotangent, input_ids, target_ids):
    shard_rows = table.shape[0]
    width = table.shape[1]
    offset = lax.axis_index("vocab") * shard_rows
    rows = lax.all_gather(hidden, "vocab", axis=0, tiled=True)
    incoming = lax.all_gather(cotangent, "vocab", axis=0, tiled=True)
    logits = lax.dot_general(
        rows, table, (((1,), (1,)), ((), ())), preferred_element_type=jnp.float32
    )
    columns = offset + jnp.arange(shard_rows, dtype=jnp.int32)
    hit = target_ids[:, None] == columns[None, :]
    local_pick = jnp.sum(jnp.where(hit, logits, jnp.float32(0.0)), axis=1)
    local_max = jnp.max(logits, axis=1)
    top = lax.pmax(local_max, "vocab")
    local_total = jnp.sum(jnp.exp(logits - top[:, None]), axis=1)
    total, picked = lax.psum((local_total, local_pick), "vocab")
    lse = top + jnp.log(total)
    token_loss = lse - picked
    dlogits = (jnp.exp(logits - lse[:, None]) - hit.astype(jnp.float32)).astype(jnp.bfloat16)
    hidden_grad = lax.psum_scatter(
        jnp.dot(dlogits, table, preferred_element_type=jnp.float32),
        "vocab",
        scatter_dimension=0,
        tiled=True,
    ).astype(jnp.bfloat16)
    local_ids = input_ids - offset
    inside = (local_ids >= 0) & (local_ids < shard_rows)
    targets = jnp.where(inside, local_ids, shard_rows)
    first_section = (
        jnp.zeros((shard_rows, width), jnp.float32)
        .at[targets]
        .add(incoming.astype(jnp.float32), mode="drop")
    )
    full = (
        lax.dot_general(dlogits, rows, (((0,), (0,)), ((), ())), preferred_element_type=jnp.float32)
        + first_section
    )
    table_grad = lax.psum_scatter(full, "dp", scatter_dimension=0, tiled=True)
    return (table_grad, hidden_grad, token_loss)


def solution(mesh):
    return jax.shard_map(
        shards,
        mesh=mesh,
        in_specs=(
            P("vocab", None),
            P(("dp", "vocab"), None),
            P(("dp", "vocab"), None),
            P("dp"),
            P("dp"),
        ),
        out_specs=(P(("vocab", "dp"), None), P(("dp", "vocab"), None), P("dp")),
        check_vma=False,
    )
```

profile of v0, /device:TPU:0, one launch (start us, length us, event | category | flops | bytes accessed | tf_op | source)
XLA Modules:
  0.0 292.8 jit_solution(14492816868424003785)
XLA Ops:
  7.2 0.0 all-gather.3.cloned.1.call-start
  7.2 0.7 all-gather.3.cloned.1.call-update
  7.9 0.0 all-gather.5.cloned.1.call-start
  7.9 0.7 all-gather.5.cloned.1.call-update
  8.6 0.0 reduce-scatter.5.cloned.1.call-start
  8.7 0.0 copy-start.1
  8.7 65.2 %all-gather.3.cloned.1.call-done = bf16[256,4096]{1,0:T(8,128)(2,1)} async-done(((bf16[16,4096]{1,0:T(8,128)(2,1)}), bf16[256,4096]{1,0:T(8,128)(2,1)}) %all-gather.3.cloned.1.call-update) | async-done | bytes 2097168 | tf_op jit(solution)/shard_map/all_gather | solution.py:11
  73.9 6.5 %fusion.10 = (f32[256]{0:T(256)S(1)}, f32[256,1024]{1,0:T(8,128)S(1)}) fusion(bf16[256,4096]{1,0:T(8,128)(2,1)} %all-gather.3.cloned.1.call-done, bf16[1024,4096]{1,0:T(8,128)(2,1)} %param.5), kind=kOutput, calls=%fused_computation.16 | convolution fusion | flops 2147745536 | bytes 11535360 | tf_op jit(solution)/shard_map/dot_general | solution.py:13
  80.3 39.8 %pmax.7 = f32[256]{0:T(256)S(1)} all-reduce(f32[256]{0:T(256)S(1)} %get-tuple-element.9), channel_id=1, replica_groups=mesh['dp'=2,'vocab'=16] {'vocab'}, use_global_device_ids=true, to_apply=%region_1.2 | all-reduce | flops 256 | bytes 2048 | tf_op jit(solution)/shard_map/pmax | solution.py:20
  120.2 0.0 copy-done.1
  120.2 0.4 fusion.4
  120.6 36.9 %all-reduce = (f32[256]{0:T(256)S(1)}, f32[256]{0:T(256)S(1)}) all-reduce(f32[256]{0:T(256)S(1)} %get-tuple-element.4, f32[256]{0:T(256)S(1)} %get-tuple-element.3), channel_id=1, replica_groups=mesh['dp'=2,'vocab'=16] {'vocab'}, use_global_device_ids=true, to_apply=%region_3.4 | all-reduce | flops 512 | bytes 4096 | tf_op jit(solution)/shard_map/psum | solution.py:22
  157.4 0.6 fusion.9
  158.0 7.8 %fusion.5 = f32[256,4096]{1,0:T(8,128)} fusion(bf16[1024,4096]{1,0:T(8,128)(2,1)} %param.5, f32[256,1024]{1,0:T(8,128)S(1)} %get-tuple-element.10, s32[1024]{0:T(1024)S(1)} %iota_add_fusion, f32[256]{0:T(256)S(1)} %get-tuple-element.8, s32[256]{0:T(256)S(1)} %copy-done.1), kind=kOutput, calls=%fused_computation.13 | convolution fusion | flops 2148794368 | bytes 13637632 | tf_op jit(solution)/shard_map/dot_general | solution.py:27
  165.8 0.0 reduce-scatter.5.cloned.1.call-update
  165.8 0.2 reduce-scatter.3.cloned.1.call-start
  166.1 0.4 copy-done.2
  166.5 0.9 copy-done
  167.4 8.2 %fusion.7 = f32[1024,4096]{1,0:T(8,128)} fusion(bf16[256,4096]{1,0:T(8,128)(2,1)S(1)} %copy-done, f32[256,1024]{1,0:T(8,128)S(1)} %get-tuple-element.10, s32[1024]{0:T(1024)S(1)} %iota_add_fusion, f32[256]{0:T(256)S(1)} %get-tuple-element.8, s32[256]{0:T(256)S(1)} %copy-done.1), kind=kOutput, calls=%fused_computation.14 | convolution fusion | flops 2148794368 | bytes 19929088 | tf_op jit(solution)/shard_map/dot_general | solution.py:41
  175.6 18.7 %scatter_custom_fusion = f32[1024,4096]{1,0:T(8,128)} fusion(f32[1024,4096]{1,0:T(8,128)} %fusion.7, s32[256]{0:T(256)S(1)} %compare_select_fusion.1, bf16[256,4096]{1,0:T(8,128)(2,1)} %all-gather.5.cloned.1.call-done), kind=kCustom, calls=%fused_computation.1 | custom fusion | flops 2097152 | bytes 18874368 | tf_op jit(solution)/shard_map/scatter-add | solution.py:38
  194.4 0.0 reduce-scatter.3.cloned.1.call-update
  194.4 64.5 %reduce-scatter.5.cloned.1.call-done = f32[16,4096]{1,0:T(8,128)} async-done(((f32[256,4096]{1,0:T(8,128)}), f32[16,4096]{1,0:T(8,128)}) %reduce-scatter.5.cloned.1.call-update) | async-done | bytes 262160 | tf_op jit(solution)/shard_map/reduce_scatter | solution.py:26
  258.9 1.6 convert_element_type.15
  260.5 25.7 %reduce-scatter.3.cloned.1.call-done = f32[512,4096]{1,0:T(8,128)} async-done(((f32[1024,4096]{1,0:T(8,128)}), f32[512,4096]{1,0:T(8,128)}) %reduce-scatter.3.cloned.1.call-update) | async-done | bytes 8388624 | tf_op jit(solution)/shard_map/reduce_scatter | solution.py:44
  (5 shorter events, 0.0 us)
Async XLA Ops:
  7.2 66.7 %all-gather.3.cloned.1.call-start = ((), (), s32[]{:S(2)}) async-start(), calls=%async_computation.2 | async-start | bytes 2228224 | tf_op jit(solution)/shard_map/all_gather | solution.py:11
  7.9 167.7 %all-gather.5.cloned.1.call-start = ((), (), s32[]{:S(2)}) async-start(), calls=%async_computation.3 | async-start | bytes 2228224 | tf_op jit(solution)/shard_map/all_gather | solution.py:12
  8.6 250.2 %reduce-scatter.5.cloned.1.call-start = ((), (), s32[]{:S(2)}) async-start(), calls=%async_computation.5 | async-start | bytes 4456448 | tf_op jit(solution)/shard_map/reduce_scatter | solution.py:26
  8.7 111.4 %copy-start.1 = (s32[256]{0:T(256)S(1)}, s32[256]{0:T(256)}, u32[]{:S(2)}) copy-start(s32[256]{0:T(256)} %param.9) | copy-start | bytes 3076
  165.8 0.7 copy-start.2
  165.8 1.6 copy-start
  165.8 120.4 %reduce-scatter.3.cloned.1.call-start = ((), (), s32[]{:S(2)}) async-start(), calls=%async_computation.4 | async-start | bytes 25165824 | tf_op jit(solution)/shard_map/reduce_scatter | solution.py:44
Sparse Core Ops, SparseCore 0:
  10.7 63.0 all-gather.2
  76.6 59.4 all-gather.4
  165.9 92.8 reduce-scatter.4
  261.6 24.5 reduce-scatter.2
where the time goes:
time: 293 us
  waiting for transfers between devices  157 us (54%)
  blocking collectives  76.7 us (26%)
  matrix products  22.5 us (8%)
  other arithmetic  21.3 us (7%)
  between operations  13.8 us (5%)
    all_gather x1, waiting for transfers between devices, shards(): rows = lax.all_gather(hidden, 'vocab', axis=0, tiled=True)  65.2 us
    reduce_scatter x1, waiting for transfers between devices, shards(): lax.psum_scatter(jnp.dot(dlogits, table, preferred_element_type=jnp.float...  64.5 us
    pmax x1, blocking collectives, shards(): top = lax.pmax(local_max, 'vocab')  39.8 us
    psum x1, blocking collectives, shards(): total, picked = lax.psum((local_total, local_pick), 'vocab')  36.9 us
    reduce_scatter x1, waiting for transfers between devices, shards(): table_grad = lax.psum_scatter(full, 'dp', scatter_dimension=0, tiled=True)  25.7 us
    scatter-add x1, other arithmetic, shards(): first_section = jnp.zeros((shard_rows, width), jnp.float32).at[targets].a...  18.7 us
    dot_general x1, matrix products, shards(): lax.dot_general(dlogits, rows, (((0,), (0,)), ((), ())), preferred_elemen...  8.23 us
    dot_general x1, matrix products, shards(): jnp.dot(dlogits, table, preferred_element_type=jnp.float32)  7.77 us
  transfers between devices with their start and end apart: 4, of which 3 were waited for; matrix products, arithmetic and copies ran while one was open for 15% of the time, Pallas kernels for 0%

commit v1 on v0

v1 whole, which is shorter than its diff:
```python
import functools

import jax
import jax.numpy as jnp
from jax import lax
from jax.experimental import pallas as pl
from jax.experimental.pallas import tpu as pltpu
from jax.sharding import PartitionSpec as P

MESH = pl.DeviceIdType.MESH
BF16 = jnp.bfloat16
F32 = jnp.float32
WIRE1 = BF16
WIRE2 = BF16
WIREZ = BF16


def kernel(groups, n, table_hbm, hidden_ref, cot_ref, in_ids_ref, tgt_ids_ref,
           x_all, e_all, hg_ref, loss_ref,
           table, x_own, logits, st, own_e, part, s1, r1, s2, r2, s3, r3,
           load_sem, local_sem, send, recv):
    nz = n // 4
    rows, width = hidden_ref.shape
    shard = table.shape[0]
    tokens = n * rows
    piece = shard // groups
    half = width // 2
    me = lax.axis_index("vocab")
    g = lax.axis_index("dp")
    z = me // 4
    y = (me % 4) // 2
    x = me % 2
    slots = iter(range(send.shape[0]))

    def at(zz, yy, xx):
        return zz * 4 + yy * 2 + xx

    x_peer = at(z, y, 1 - x)
    y_peer = at(z, 1 - y, x)

    load = pltpu.make_async_copy(table_hbm, table, load_sem)
    load.start()

    barrier = pltpu.get_barrier_semaphore()
    for d in range(1, n):
        pl.semaphore_signal(barrier, inc=1, device_id=(g, (me + d) % n), device_id_type=MESH)
    for d in range(1, groups):
        pl.semaphore_signal(barrier, inc=1, device_id=((g + d) % groups, me), device_id_type=MESH)
    pl.semaphore_wait(barrier, n - 1 + groups - 1)

    started = []

    def push(src, dst, v, gg=None):
        k = next(slots)
        c = pltpu.make_async_remote_copy(
            src_ref=src, dst_ref=dst, send_sem=send.at[k], recv_sem=recv.at[k],
            device_id=(g if gg is None else gg, v), device_id_type=MESH)
        c.start()
        started.append(c)
        return c

    left = pl.ds(0, half)
    right = pl.ds(half, half)

    def gather_first(kind, own):
        dst = x_own.at[kind, me]
        fx = [push(own, dst, x_peer)]
        fy = [push(own, dst, y_peer)]
        fz = [push(own, dst, at((z + d) % nz, y, x)) for d in range(1, nz)]
        return fx, fy, fz

    def gather_second(kind, state):
        fx, fy, fz = state
        for d in range(1, nz):
            fz[d - 1].wait_recv()
            blk = x_own.at[kind, at((z + nz - d) % nz, y, x)]
            fx.append(push(blk, blk, x_peer))
            fy.append(push(blk, blk, y_peer))

    def gather_third(kind, state):
        fx, fy, _ = state
        out = []
        for d in range(nz):
            zz = (z + nz - d) % nz
            fx[d].wait_recv()
            blk = x_own.at[kind, at(zz, y, 1 - x), :, left]
            out.append(push(blk, blk, y_peer))
            fy[d].wait_recv()
            blk = x_own.at[kind, at(zz, 1 - y, x), :, right]
            out.append(push(blk, blk, x_peer))
        return out

    local = []

    def spread(kind):
        c = pltpu.make_async_copy(x_own.at[kind], x_all.at[g, kind], local_sem.at[kind])
        c.start()
        local.append(c)
        return [push(x_own.at[kind], x_all.at[g, kind], me, (g + d) % groups) for d in range(1, groups)]

    state = gather_first(0, hidden_ref)
    x_own[0, pl.ds(me, 1)] = hidden_ref[...][None]
    x_own[1, pl.ds(me, 1)] = cot_ref[...][None]
    gather_second(0, state)
    tail = gather_third(0, state)
    cot_state = gather_first(1, cot_ref)
    offset = me * shard
    step = 256
    for i in range(0, shard, step):
        vocab_row = offset + i + lax.broadcasted_iota(jnp.int32, (step, tokens), 0)
        own_e[1, i:i + step] = (vocab_row == in_ids_ref[...]).astype(F32).astype(BF16)
    for c in tail:
        c.wait_recv()
    late = spread(0)
    load.wait()
    h = x_own[0].reshape(tokens, width)
    top = jnp.full((1, tokens), -jnp.inf, F32)
    for i in range(0, shard, step):
        lg = lax.dot_general(table[i:i + step], h, (((1,), (1,)), ((), ())), preferred_element_type=F32)
        logits[i:i + step] = lg
        top = jnp.maximum(top, jnp.max(lg, axis=0, keepdims=True))
    total = jnp.zeros((1, tokens), F32)
    pick = jnp.zeros((1, tokens), F32)
    tgt = tgt_ids_ref[...]
    for i in range(0, shard, step):
        lg = logits[i:i + step]
        vocab_row = offset + i + lax.broadcasted_iota(jnp.int32, (step, tokens), 0)
        total = total + jnp.sum(jnp.exp(lg - top), axis=0, keepdims=True)
        pick = pick + jnp.sum(jnp.where(vocab_row == tgt, lg, 0.0), axis=0, keepdims=True)
    line = lax.broadcasted_iota(jnp.int32, (8, tokens), 0)
    mine = jnp.where(line == 0, top, jnp.where(line == 1, total, pick))
    st[pl.ds(me, 1)] = mine[None]
    stats = [push(st.at[me], st.at[me], (me + d) % n) for d in range(1, n)]
    gather_second(1, cot_state)
    for c in stats:
        c.wait_recv()
    top = st[0, 0:1]
    for j in range(1, n):
        top = jnp.maximum(top, st[j, 0:1])
    total = jnp.zeros((1, tokens), F32)
    pick = jnp.zeros((1, tokens), F32)
    for j in range(n):
        total = total + st[j, 1:2] * jnp.exp(st[j, 0:1] - top)
        pick = pick + st[j, 2:3]
    lse = top + jnp.log(total)
    loss_ref[...] = lse - pick
    for i in range(0, shard, step):
        vocab_row = offset + i + lax.broadcasted_iota(jnp.int32, (step, tokens), 0)
        hit = (vocab_row == tgt).astype(F32)
        own_e[0, i:i + step] = (jnp.exp(logits[i:i + step] - lse) - hit).astype(BF16)

    dl = own_e[0]
    cols = 512

    def product(i):
        p = lax.dot_general(dl, table[:, i:i + cols], (((0,), (0,)), ((), ())), preferred_element_type=F32)
        part[:, :, :, :, i:i + cols] = p.reshape(nz, 2, 2, rows, cols)

    for i in range(0, half, cols):
        product(i)
    s1[0] = part[:, pl.ds(1 - y, 1), :, :, 0:half].reshape(nz, 2, rows, half).astype(WIRE1)
    ca = push(s1.at[0], r1.at[0], y_peer)
    for i in range(half, width, cols):
        product(i)
    s1[1] = part[:, :, pl.ds(1 - x, 1), :, half:width].reshape(nz, 2, rows, half).astype(WIRE1)
    cb = push(s1.at[1], r1.at[1], x_peer)

    for kind in range(2):
        dst = e_all.at[:, pl.ds(pl.multiple_of((g * 2 + kind) * tokens, tokens), tokens)]
        c = pltpu.make_async_copy(
            own_e.at[kind, pl.ds(pl.multiple_of(g * piece, piece), piece)], dst, local_sem.at[2 + kind])
        c.start()
        local.append(c)
        for d in range(1, groups):
            peer = (g + d) % groups
            late.append(push(own_e.at[kind, pl.ds(pl.multiple_of(peer * piece, piece), piece)], dst, me, peer))

    cot_tail = gather_third(1, cot_state)

    ca.wait_recv()
    s2[0] = (part[:, pl.ds(y, 1), pl.ds(1 - x, 1), :, 0:half].reshape(nz, rows, half)
             + r1[0, :, pl.ds(1 - x, 1)].reshape(nz, rows, half).astype(F32)).astype(WIRE2)
    da = push(s2.at[0], r2.at[0], x_peer)
    cb.wait_recv()
    s2[1] = (part[:, pl.ds(1 - y, 1), pl.ds(x, 1), :, half:width].reshape(nz, rows, half)
             + r1[1, :, pl.ds(1 - y, 1)].reshape(nz, rows, half).astype(F32)).astype(WIRE2)
    db = push(s2.at[1], r2.at[1], y_peer)

    def merged(side, zz):
        a = part[pl.ds(zz, 1), pl.ds(y, 1), pl.ds(x, 1), :, side * half:(side + 1) * half].reshape(rows, half)
        b = r1[side, pl.ds(zz, 1), pl.ds(x if side == 0 else y, 1)].reshape(rows, half).astype(F32)
        return a + b + r2[side, pl.ds(zz, 1)].reshape(rows, half).astype(F32)

    last = []
    for side, c in ((0, da), (1, db)):
        c.wait_recv()
        for d in range(1, nz):
            zz = (z + d) % nz
            s3[side, d - 1] = merged(side, zz).astype(WIREZ)
            last.append(push(s3.at[side, d - 1], r3.at[side, d - 1], at(zz, y, x)))
    for c in cot_tail:
        c.wait_recv()
    late += spread(1)
    for c in last:
        c.wait_recv()
    for side in range(2):
        acc = merged(side, z)
        for d in range(1, nz):
            acc = acc + r3[side, d - 1].astype(F32)
        hg_ref[:, side * half:(side + 1) * half] = acc.astype(BF16)
    for c in late:
        c.wait_recv()
    for c in local:
        c.wait()
    for c in started:
        c.wait_send()


def solution(mesh):
    groups, n = mesh.shape["dp"], mesh.shape["vocab"]

    def body(table, hidden, cotangent, input_ids, target_ids):
        rows, width = hidden.shape
        shard = table.shape[0]
        nz = n // 4
        tokens = n * rows
        half = width // 2
        piece = shard // groups
        copies = 2 * (nz + 1 + 2 * (nz - 1) + 2 * nz) + 2 * (groups - 1) + (n - 1) + 2 + 2 * (groups - 1) + 2 + 2 * (nz - 1)
        vmem = pl.BlockSpec(memory_space=pltpu.VMEM)
        anys = pl.BlockSpec(memory_space=pl.ANY)
        x_all, e_all, hg, loss = pl.pallas_call(
            functools.partial(kernel, groups, n),
            out_shape=(
                jax.ShapeDtypeStruct((groups, 2, n, rows, width), BF16),
                jax.ShapeDtypeStruct((piece, groups * 2 * tokens), BF16),
                jax.ShapeDtypeStruct((rows, width), BF16),
                jax.ShapeDtypeStruct((1, tokens), F32),
            ),
            in_specs=[anys, vmem, vmem, vmem, vmem],
            out_specs=(anys, anys, vmem, vmem),
            scratch_shapes=[
                pltpu.VMEM((shard, width), BF16),
                pltpu.VMEM((2, n, rows, width), BF16),
                pltpu.VMEM((shard, tokens), F32),
                pltpu.VMEM((n, 8, tokens), F32),
                pltpu.VMEM((2, shard, tokens), BF16),
                pltpu.VMEM((nz, 2, 2, rows, width), F32),
                pltpu.VMEM((2, nz, 2, rows, half), WIRE1),
                pltpu.VMEM((2, nz, 2, rows, half), WIRE1),
                pltpu.VMEM((2, nz, rows, half), WIRE2),
                pltpu.VMEM((2, nz, rows, half), WIRE2),
                pltpu.VMEM((2, nz - 1, rows, half), WIREZ),
                pltpu.VMEM((2, nz - 1, rows, half), WIREZ),
                pltpu.SemaphoreType.DMA,
                pltpu.SemaphoreType.DMA((4,)),
                pltpu.SemaphoreType.DMA((copies,)),
                pltpu.SemaphoreType.DMA((copies,)),
            ],
            compiler_params=pltpu.CompilerParams(
                collective_id=0, has_side_effects=True, vmem_limit_bytes=56 * 2**20),
        )(table, hidden, cotangent, input_ids.reshape(1, tokens), target_ids.reshape(1, tokens))
        table_grad = jnp.dot(
            e_all, x_all.reshape(groups * 2 * tokens, width), preferred_element_type=F32)
        return table_grad, hg, loss.reshape(tokens)

    return jax.shard_map(
        body,
        mesh=mesh,
        in_specs=(
            P("vocab", None),
            P(("dp", "vocab"), None),
            P(("dp", "vocab"), None),
            P("dp"),
            P("dp"),
        ),
        out_specs=(P(("vocab", "dp"), None), P(("dp", "vocab"), None), P("dp")),
        check_vma=False,
    )
```

time: 293 us -> 92.4 us (0.32)
  waiting for transfers between devices: 157 us -> 0 us
  Pallas kernels: 0 us -> 78.8 us
  blocking collectives: 76.7 us -> 0 us
  other arithmetic: 21.3 us -> 0 us
  between operations: 13.8 us -> 0.66 us
  matrix products: 22.5 us -> 11.6 us
    reduce_scatter x2 -> x0, waiting for transfers between devices: 90.2 us -> none  [the longest x1 64.5 us: shards(): lax.psum_scatter(jnp.dot(dlogits, table, preferred_element_type=jnp.float...]
    pallas_call x0 -> x1, Pallas kernels: none -> 78.8 us  [body(): pl.pallas_call(functools.partial(kernel, groups, n), out_shape=(jax.Shape...]
    all_gather x2 -> x0, waiting for transfers between devices: 65.2 us -> none  [the longest x1 65.2 us: shards(): rows = lax.all_gather(hidden, 'vocab', axis=0, tiled=True)]
    pmax x1 -> x0, blocking collectives: 39.8 us -> none  [shards(): top = lax.pmax(local_max, 'vocab')]
    psum x1 -> x0, blocking collectives: 36.9 us -> none  [shards(): total, picked = lax.psum((local_total, local_pick), 'vocab')]
    scatter-add x1 -> x0, other arithmetic: 18.7 us -> none  [shards(): first_section = jnp.zeros((shard_rows, width), jnp.float32).at[targets].a...]
    dot_general x3 -> x1, matrix products: 22.5 us -> 11.6 us  [body(): jnp.dot(e_all, x_all.reshape(groups * 2 * tokens, width), preferred_eleme...]
  transfers between devices with their start and end apart: 4 -> 0, of which waited for: 3 -> 0; matrix products, arithmetic and copies ran while one was open for 15% -> 0% of each run, Pallas kernels for 0% -> 0%
where the time goes in v1:
time: 92.4 us; the launch traced here: 92.3 us
  Pallas kernels  78.8 us (85%)
  matrix products  11.6 us (13%)
  local copies, waits for them, and re-layouts  1.23 us (1%)
    pallas_call x1, Pallas kernels, body(): pl.pallas_call(functools.partial(kernel, groups, n), out_shape=(jax.Shape...  78.8 us
    dot_general x1, matrix products, body(): jnp.dot(e_all, x_all.reshape(groups * 2 * tokens, width), preferred_eleme...  11.6 us

profile of v1, /device:TPU:0, one launch (start us, length us, event | category | flops | bytes accessed | tf_op | source)
XLA Modules:
  0.0 92.3 jit_solution(11782920008628428659)
XLA Ops:
  0.6 78.8 %shard_map.76 = (bf16[2,2,16,16,4096]{4,3,2,1,0:T(8,128)(2,1)}, bf16[512,1024]{1,0:T(8,128)(2,1)}, bf16[16,4096]{1,0:T(8,128)(2,1)}, f32[1,256]{1,0:T(1,128)}) custom-call(bf16[1024,4096]{1,0:T(8,128)(2,1)} %table_hbm.1, bf16[16,4096]{1,0:T(8,128)(2,1)} %hidden_ref.1, bf16[16,4096]{1,0:T(8,128)(2,1)} %cot_ref.1, s32[1,256]{1,0:T(1,128)} %bitcast.6, ...), custom_call_target="tpu_custom_call" | custom-call | tf_op jit(solution)/shard_map/pallas_call | solution.py:232
  79.4 0.0 copy-start
  79.4 0.0 copy-start.1
  79.4 11.6 %fusion = f32[512,4096]{1,0:T(8,128)} fusion(bf16[512,1024]{1,0:T(8,128)(2,1)} %get-tuple-element.7, bf16[1024,4096]{1,0:T(8,128)(2,1)} %bitcast.9), kind=kOutput, calls=%fused_computation | convolution fusion | flops 4294967296 | bytes 17825792 | tf_op jit(solution)/shard_map/dot_general | solution.py:263
  91.1 0.0 copy-done
  91.1 0.7 copy.10
  91.7 0.0 copy-done.1
  91.7 0.6 copy.11
Async XLA Ops:
  79.4 11.7 %copy-start = (bf16[16,4096]{1,0:T(8,128)(2,1)S(1)}, bf16[16,4096]{1,0:T(8,128)(2,1)}, u32[]{:S(2)}) copy-start(bf16[16,4096]{1,0:T(8,128)(2,1)} %get-tuple-element.15) | copy-start | bytes 393220
  79.4 12.3 %copy-start.1 = (f32[1,256]{1,0:T(1,128)S(1)}, f32[1,256]{1,0:T(1,128)}, u32[]{:S(2)}) copy-start(f32[1,256]{1,0:T(1,128)} %get-tuple-element.10) | copy-start | bytes 3076

commit v2 on v1

v2 whole, which is shorter than its diff:
```python
import functools

import jax
import jax.numpy as jnp
from jax import lax
from jax.experimental import pallas as pl
from jax.experimental.pallas import tpu as pltpu
from jax.sharding import PartitionSpec as P

MESH = pl.DeviceIdType.MESH
BF16 = jnp.bfloat16
F32 = jnp.float32
WIRE1 = BF16
WIRE2 = BF16
WIREZ = BF16
CHUNKS = 2


def kernel(groups, n, table_hbm, hidden_ref, cot_ref, in_ids_ref, tgt_ids_ref,
           x_all, e_all, hg_ref, loss_ref,
           table, x_own, logits, st, own_e, part, s1, r1, s2, r2, s3, r3,
           load_sem, local_sem, send, recv):
    nz = n // 4
    rows, width = hidden_ref.shape
    shard = table.shape[0]
    tokens = n * rows
    piece = shard // groups
    half = width // 2
    me = lax.axis_index("vocab")
    g = lax.axis_index("dp")
    z = me // 4
    y = (me % 4) // 2
    x = me % 2
    slots = iter(range(send.shape[0]))

    def at(zz, yy, xx):
        return zz * 4 + yy * 2 + xx

    x_peer = at(z, y, 1 - x)
    y_peer = at(z, 1 - y, x)

    load = pltpu.make_async_copy(table_hbm, table, load_sem)
    load.start()

    barrier = pltpu.get_barrier_semaphore()
    for d in range(1, n):
        pl.semaphore_signal(barrier, inc=1, device_id=(g, (me + d) % n), device_id_type=MESH)
    for d in range(1, groups):
        pl.semaphore_signal(barrier, inc=1, device_id=((g + d) % groups, me), device_id_type=MESH)
    pl.semaphore_wait(barrier, n - 1 + groups - 1)

    started = []

    def when(cond, act):
        if cond is None:
            act()
        else:
            pl.when(cond)(act)

    def both(a, b):
        return b if a is None else jnp.logical_and(a, b)

    def push(src, dst, v, gg=None, cond=None):
        k = next(slots)
        c = pltpu.make_async_remote_copy(
            src_ref=src, dst_ref=dst, send_sem=send.at[k], recv_sem=recv.at[k],
            device_id=(g if gg is None else gg, v), device_id_type=MESH)
        when(cond, c.start)
        started.append((cond, c))
        return c

    above, below = z + 1 < nz, z > 0
    up, down = at(jnp.minimum(z + 1, nz - 1), y, x), at(jnp.maximum(z - 1, 0), y, x)

    def gather_first(kind, own, base, span):
        own = own.at[:, pl.ds(base, span)]
        dst = x_own.at[kind, me, :, pl.ds(base, span)]
        ups = push(own, dst, up, cond=above)
        downs = push(own, dst, down, cond=below)
        return [(None, z, push(own, dst, x_peer), push(own, dst, y_peer))], ups, downs, kind, base, span

    def gather_second(state):
        seen, ups, downs, kind, base, span = state
        for s in range(nz - 1):
            for inward, cond, zz, go, nxt in ((ups, z - 1 - s >= 0, jnp.maximum(z - 1 - s, 0), above, up),
                                              (downs, z + 1 + s < nz, jnp.minimum(z + 1 + s, nz - 1), below, down)):
                when(cond, inward.wait_recv)
                blk = x_own.at[kind, at(zz, y, x), :, pl.ds(base, span)]
                if s < nz - 2:
                    c = push(blk, blk, nxt, cond=both(cond, go))
                    if nxt is up:
                        ups = c
                    else:
                        downs = c
                seen.append((cond, zz, push(blk, blk, x_peer, cond=cond), push(blk, blk, y_peer, cond=cond)))

    def gather_third(state):
        seen, _, _, kind, base, span = state
        left = pl.ds(base, span // 2)
        right = pl.ds(base + span // 2, span // 2)
        out = []
        for cond, zz, fx, fy in seen:
            when(cond, fx.wait_recv)
            blk = x_own.at[kind, at(zz, y, 1 - x), :, left]
            out.append((cond, push(blk, blk, y_peer, cond=cond)))
            when(cond, fy.wait_recv)
            blk = x_own.at[kind, at(zz, 1 - y, x), :, right]
            out.append((cond, push(blk, blk, x_peer, cond=cond)))
        return out

    local = []

    def spread(kind):
        c = pltpu.make_async_copy(x_own.at[kind], x_all.at[g, kind], local_sem.at[kind])
        c.start()
        local.append(c)
        return [push(x_own.at[kind], x_all.at[g, kind], me, (g + d) % groups) for d in range(1, groups)]

    states = [gather_first(0, hidden_ref, i * half, half) for i in range(2)]
    x_own[0, pl.ds(me, 1)] = hidden_ref[...][None]
    x_own[1, pl.ds(me, 1)] = cot_ref[...][None]
    tails = []
    for state in states:
        gather_second(state)
        tails.append(gather_third(state))
    cot_state = gather_first(1, cot_ref, 0, width)
    offset = me * shard
    step = 256
    for i in range(0, shard, step):
        vocab_row = offset + i + lax.broadcasted_iota(jnp.int32, (step, tokens), 0)
        own_e[1, i:i + step] = (vocab_row == in_ids_ref[...]).astype(F32).astype(BF16)
    load.wait()
    top = jnp.full((1, tokens), -jnp.inf, F32)
    for k in range(2):
        for cond, c in tails[k]:
            when(cond, c.wait_recv)
        h = x_own[0, :, :, k * half:(k + 1) * half].reshape(tokens, half)
        for i in range(0, shard, step):
            lg = lax.dot_general(table[i:i + step, k * half:(k + 1) * half], h, (((1,), (1,)), ((), ())),
                                 preferred_element_type=F32)
            if k == 1:
                lg = lg + logits[i:i + step]
                top = jnp.maximum(top, jnp.max(lg, axis=0, keepdims=True))
            logits[i:i + step] = lg
    late = spread(0)
    total = jnp.zeros((1, tokens), F32)
    pick = jnp.zeros((1, tokens), F32)
    tgt = tgt_ids_ref[...]
    for i in range(0, shard, step):
        lg = logits[i:i + step]
        vocab_row = offset + i + lax.broadcasted_iota(jnp.int32, (step, tokens), 0)
        total = total + jnp.sum(jnp.exp(lg - top), axis=0, keepdims=True)
        pick = pick + jnp.sum(jnp.where(vocab_row == tgt, lg, 0.0), axis=0, keepdims=True)
    line = lax.broadcasted_iota(jnp.int32, (8, tokens), 0)
    mine = jnp.where(line == 0, top, jnp.where(line == 1, total, pick))
    st[pl.ds(me, 1)] = mine[None]
    stats = [push(st.at[me], st.at[me], (me + d) % n) for d in range(1, n)]
    gather_second(cot_state)
    for c in stats:
        c.wait_recv()
    top = st[0, 0:1]
    for j in range(1, n):
        top = jnp.maximum(top, st[j, 0:1])
    total = jnp.zeros((1, tokens), F32)
    pick = jnp.zeros((1, tokens), F32)
    for j in range(n):
        total = total + st[j, 1:2] * jnp.exp(st[j, 0:1] - top)
        pick = pick + st[j, 2:3]
    lse = top + jnp.log(total)
    loss_ref[...] = lse - pick
    for i in range(0, shard, step):
        vocab_row = offset + i + lax.broadcasted_iota(jnp.int32, (step, tokens), 0)
        hit = (vocab_row == tgt).astype(F32)
        own_e[0, i:i + step] = (jnp.exp(logits[i:i + step] - lse) - hit).astype(BF16)

    dl = own_e[0]
    cols = 512

    def product(i):
        p = lax.dot_general(dl, table[:, i:i + cols], (((0,), (0,)), ((), ())), preferred_element_type=F32)
        part[:, :, :, :, i:i + cols] = p.reshape(nz, 2, 2, rows, cols)

    wide = half // CHUNKS
    firsts = [[], []]
    for c in range(CHUNKS):
        for side in range(2):
            lo = side * half + c * wide
            for i in range(lo, lo + wide, cols):
                product(i)
            if side == 0:
                p = part[:, pl.ds(1 - y, 1), :, :, lo:lo + wide]
            else:
                p = part[:, :, pl.ds(1 - x, 1), :, lo:lo + wide]
            s1[side, c] = p.reshape(nz, 2, rows, wide).astype(WIRE1)
            firsts[side].append(push(s1.at[side, c], r1.at[side, c], y_peer if side == 0 else x_peer))

    for kind in range(2):
        dst = e_all.at[:, pl.ds(pl.multiple_of((g * 2 + kind) * tokens, tokens), tokens)]
        c = pltpu.make_async_copy(
            own_e.at[kind, pl.ds(pl.multiple_of(g * piece, piece), piece)], dst, local_sem.at[2 + kind])
        c.start()
        local.append(c)
        for d in range(1, groups):
            peer = (g + d) % groups
            late.append(push(own_e.at[kind, pl.ds(pl.multiple_of(peer * piece, piece), piece)], dst, me, peer))

    def merged_first(side, c, zz, yy, xx, count):
        lo = side * half + c * wide
        a = part[pl.ds(zz, count), pl.ds(yy, 1), pl.ds(xx, 1), :, lo:lo + wide].reshape(count, rows, wide)
        b = r1[side, c, pl.ds(zz, count), pl.ds(xx if side == 0 else yy, 1)].reshape(count, rows, wide)
        return a + b.astype(F32)

    seconds = [[], []]
    for c in range(CHUNKS):
        for side in range(2):
            firsts[side][c].wait_recv()
            yy, xx, peer = (y, 1 - x, x_peer) if side == 0 else (1 - y, x, y_peer)
            s2[side, c] = merged_first(side, c, 0, yy, xx, nz).astype(WIRE2)
            seconds[side].append(push(s2.at[side, c], r2.at[side, c], peer))

    cot_tail = gather_third(cot_state)

    def merged(side, c, zz):
        return (merged_first(side, c, zz, y, x, 1)
                + r2[side, c, pl.ds(zz, 1)].astype(F32)).reshape(rows, wide)

    last = []
    for c in range(CHUNKS):
        for side in range(2):
            seconds[side][c].wait_recv()
            for d in range(1, nz):
                zz = (z + d) % nz
                s3[side, c, d - 1] = merged(side, c, zz).astype(WIREZ)
                last.append(push(s3.at[side, c, d - 1], r3.at[side, c, d - 1], at(zz, y, x)))
    for cond, c in cot_tail:
        when(cond, c.wait_recv)
    late += spread(1)
    for c in last:
        c.wait_recv()
    for c in range(CHUNKS):
        for side in range(2):
            acc = merged(side, c, z)
            for d in range(1, nz):
                acc = acc + r3[side, c, d - 1].astype(F32)
            lo = side * half + c * wide
            hg_ref[:, lo:lo + wide] = acc.astype(BF16)
    for c in late:
        c.wait_recv()
    for c in local:
        c.wait()
    for cond, c in started:
        when(cond, c.wait_send)


def weight_kernel(e_ref, x_ref, out_ref):
    out_ref[...] = jnp.dot(e_ref[...], x_ref[...], preferred_element_type=F32)


def weight_grad(e, x):
    tile = 512
    return pl.pallas_call(
        weight_kernel,
        grid=(x.shape[1] // tile,),
        out_shape=jax.ShapeDtypeStruct((e.shape[0], x.shape[1]), F32),
        in_specs=[
            pl.BlockSpec(e.shape, lambda i: (0, 0)),
            pl.BlockSpec((x.shape[0], tile), lambda i: (0, i)),
        ],
        out_specs=pl.BlockSpec((e.shape[0], tile), lambda i: (0, i)),
        compiler_params=pltpu.CompilerParams(vmem_limit_bytes=60 * 2**20),
    )(e, x)


def solution(mesh):
    groups, n = mesh.shape["dp"], mesh.shape["vocab"]

    def body(table, hidden, cotangent, input_ids, target_ids):
        rows, width = hidden.shape
        shard = table.shape[0]
        nz = n // 4
        tokens = n * rows
        half = width // 2
        piece = shard // groups
        copies = 3 * (4 + 2 * (nz - 2) + 8 * (nz - 1) + 2) + 2 * (groups - 1) + (n - 1) + 2 * (groups - 1) + CHUNKS * (4 + 2 * (nz - 1))
        wide = half // CHUNKS
        vmem = pl.BlockSpec(memory_space=pltpu.VMEM)
        anys = pl.BlockSpec(memory_space=pl.ANY)
        x_all, e_all, hg, loss = pl.pallas_call(
            functools.partial(kernel, groups, n),
            out_shape=(
                jax.ShapeDtypeStruct((groups, 2, n, rows, width), BF16),
                jax.ShapeDtypeStruct((piece, groups * 2 * tokens), BF16),
                jax.ShapeDtypeStruct((rows, width), BF16),
                jax.ShapeDtypeStruct((1, tokens), F32),
            ),
            in_specs=[anys, vmem, vmem, vmem, vmem],
            out_specs=(anys, anys, vmem, vmem),
            scratch_shapes=[
                pltpu.VMEM((shard, width), BF16),
                pltpu.VMEM((2, n, rows, width), BF16),
                pltpu.VMEM((shard, tokens), F32),
                pltpu.VMEM((n, 8, tokens), F32),
                pltpu.VMEM((2, shard, tokens), BF16),
                pltpu.VMEM((nz, 2, 2, rows, width), F32),
                pltpu.VMEM((2, CHUNKS, nz, 2, rows, wide), WIRE1),
                pltpu.VMEM((2, CHUNKS, nz, 2, rows, wide), WIRE1),
                pltpu.VMEM((2, CHUNKS, nz, rows, wide), WIRE2),
                pltpu.VMEM((2, CHUNKS, nz, rows, wide), WIRE2),
                pltpu.VMEM((2, CHUNKS, nz - 1, rows, wide), WIREZ),
                pltpu.VMEM((2, CHUNKS, nz - 1, rows, wide), WIREZ),
                pltpu.SemaphoreType.DMA,
                pltpu.SemaphoreType.DMA((4,)),
                pltpu.SemaphoreType.DMA((copies,)),
                pltpu.SemaphoreType.DMA((copies,)),
            ],
            compiler_params=pltpu.CompilerParams(
                collective_id=0, has_side_effects=True, vmem_limit_bytes=56 * 2**20),
        )(table, hidden, cotangent, input_ids.reshape(1, tokens), target_ids.reshape(1, tokens))
        table_grad = weight_grad(e_all, x_all.reshape(groups * 2 * tokens, width))
        return table_grad, hg, loss.reshape(tokens)

    return jax.shard_map(
        body,
        mesh=mesh,
        in_specs=(
            P("vocab", None),
            P(("dp", "vocab"), None),
            P(("dp", "vocab"), None),
            P("dp"),
            P("dp"),
        ),
        out_specs=(P(("vocab", "dp"), None), P(("dp", "vocab"), None), P("dp")),
        check_vma=False,
    )
```

time: 92.4 us -> 85.8 us (0.929)
  matrix products: 11.6 us -> 0 us
  Pallas kernels: 78.8 us -> 83.6 us
    dot_general x1 -> x0, matrix products: 11.6 us -> none  [body(): jnp.dot(e_all, x_all.reshape(groups * 2 * tokens, width), preferred_eleme...]
    pallas_call x0 -> x1, Pallas kernels: none -> 11.2 us  [weight_grad(): pl.pallas_call(weight_kernel, grid=(x.shape[1] // tile,), out_shape=jax.S...]
    pallas_call x1, Pallas kernels: 78.8 us -> 72.4 us  [body(): pl.pallas_call(functools.partial(kernel, groups, n), out_shape=(jax.Shape...]
where the time goes in v2:
time: 85.8 us; the launch traced here: 85.4 us
  Pallas kernels  83.6 us (97%)
  local copies, waits for them, and re-layouts  1.23 us (1%)
    pallas_call x1, Pallas kernels, body(): pl.pallas_call(functools.partial(kernel, groups, n), out_shape=(jax.Shape...  72.4 us
    pallas_call x1, Pallas kernels, weight_grad(): pl.pallas_call(weight_kernel, grid=(x.shape[1] // tile,), out_shape=jax.S...  11.2 us

profile of v2, /device:TPU:0, one launch (start us, length us, event | category | flops | bytes accessed | tf_op | source)
XLA Modules:
  0.0 85.4 jit_solution(11034349734399259251)
XLA Ops:
  0.6 72.4 %shard_map.76 = (bf16[2,2,16,16,4096]{4,3,2,1,0:T(8,128)(2,1)}, bf16[512,1024]{1,0:T(8,128)(2,1)}, bf16[16,4096]{1,0:T(8,128)(2,1)}, f32[1,256]{1,0:T(1,128)}) custom-call(bf16[1024,4096]{1,0:T(8,128)(2,1)} %table_hbm.1, bf16[16,4096]{1,0:T(8,128)(2,1)} %hidden_ref.1, bf16[16,4096]{1,0:T(8,128)(2,1)} %cot_ref.1, s32[1,256]{1,0:T(1,128)} %bitcast.5, ...), custom_call_target="tpu_custom_call" | custom-call | tf_op jit(solution)/shard_map/pallas_call | solution.py:288
  73.0 0.0 copy-start
  73.0 0.0 copy-start.1
  73.0 11.2 %shard_map.77 = f32[512,4096]{1,0:T(8,128)} custom-call(bf16[512,1024]{1,0:T(8,128)(2,1)} %get-tuple-element.7.e_ref, bf16[1024,4096]{1,0:T(8,128)(2,1)} %bitcast.4), custom_call_target="tpu_custom_call" | custom-call | tf_op jit(solution)/shard_map/pallas_call | solution.py:261
  84.2 0.0 copy-done
  84.2 0.7 copy.10
  84.9 0.0 copy-done.1
  84.9 0.6 copy.11
Async XLA Ops:
  73.0 11.2 %copy-start = (bf16[16,4096]{1,0:T(8,128)(2,1)S(1)}, bf16[16,4096]{1,0:T(8,128)(2,1)}, u32[]{:S(2)}) copy-start(bf16[16,4096]{1,0:T(8,128)(2,1)} %get-tuple-element.15) | copy-start | bytes 393220
  73.0 11.8 %copy-start.1 = (f32[1,256]{1,0:T(1,128)S(1)}, f32[1,256]{1,0:T(1,128)}, u32[]{:S(2)}) copy-start(f32[1,256]{1,0:T(1,128)} %get-tuple-element.10) | copy-start | bytes 3076
